TPU v7x, 32 devices: a whole 2x2x4 slice. The times are simulated.
32 devices in a mesh: league: 2 (over x), seq: 16 (over z, y, core).
Axes of the slice: x: 2, y: 2, z: 4, core: 2. Of those that a mesh axis runs over, the one named last changes fastest.
Arguments:
- queries: bfloat16 [6144, 1792], P(('league', 'seq')), parts along dimension 0, may hold values from -100 to 100
- key_rows: bfloat16 [6144, 256], P(('league', 'seq')), parts along dimension 0, may hold values from -4 to 4
- value_rows: bfloat16 [6144, 256], P(('league', 'seq')), parts along dimension 0, may hold values from -6 to 6
- residual: bfloat16 [6144, 3584], P(('league', 'seq')), parts along dimension 0, may hold values from -6 to 6
- out_weight: bfloat16 [1792, 3584], P('seq'), may hold values from -0.125 to 0.125
- norm_gain: float32 [3584], replicated, may hold values from 0.1 to 1.9
- value_head: float32 [3584], replicated, may hold values from -0.09375 to 0.09375
- valid_length: int32 [2], P('league'), parts along dimension 0, may hold values from 1537 to 3072
Outputs:
- stream: bfloat16 [6144, 3584], P(('league', 'seq')), parts along dimension 0
- values: float32 [6144], P(('league', 'seq')), parts along dimension 0
There are 2 independent parts, one for each index of `league`. A program takes and returns all parts, laid end to end along the dimension named above; an argument that names none is the same for every part. Nothing has to cross between parts.
All inputs are finite; a program needn't handle non-finite values.
Results may differ from a plain program's by a relative error of at most 0.0085.
Values may be sent and summed in bfloat16 or wider, within the bound.
A program may use at most 128 MiB of HBM per device.

v0:
```python
import math
import jax
import jax.numpy as jnp
from jax import lax
from jax.sharding import PartitionSpec as P

HEAD_DIM = 128
NEG_BIG = -1e30


def row_positions(row_index, tok_count):
    owner_dev = row_index // tok_count
    within = row_index % tok_count
    return owner_dev * tok_count + within


def attend_block(
    carried, key_block, value_block, key_pos, query_grid, query_pos, query_limit, score_scale
):

    def run_block(carry_in):
        running_max, running_sum, running_out = carry_in
        scores = (
            jnp.einsum("qgrd,kgd->qgrk", query_grid, key_block, preferred_element_type=jnp.float32)
            * score_scale
        )
        allowed = key_pos[None, None, None, :] <= query_pos[:, None, None, None]
        new_max = jnp.maximum(running_max, jnp.max(jnp.where(allowed, scores, NEG_BIG), axis=-1))
        shrink = jnp.exp(running_max - new_max)
        weights = jnp.where(allowed, jnp.exp(scores - new_max[..., None]), 0.0)
        running_sum = running_sum * shrink + jnp.sum(weights, axis=-1)
        running_out = running_out * shrink[..., None] + jnp.einsum(
            "qgrk,kgd->qgrd",
            weights.astype(jnp.bfloat16),
            value_block,
            preferred_element_type=jnp.float32,
        )
        return (new_max, running_sum, running_out)

    def keep_block(carry_in):
        return carry_in

    needed = jnp.min(key_pos) <= query_limit
    return lax.cond(needed, run_block, keep_block, carried)


def attend_piece(
    carried, key_piece, value_piece, key_pos, query_grid, query_pos, query_limit, score_scale
):
    piece_rows = key_piece.shape[0]
    block_rows = math.gcd(piece_rows, 512)
    block_count = piece_rows // block_rows
    groups = key_piece.shape[1] // HEAD_DIM
    key_blocks = key_piece.reshape(block_count, block_rows, groups, HEAD_DIM)
    value_blocks = value_piece.reshape(block_count, block_rows, groups, HEAD_DIM)
    pos_blocks = key_pos.reshape(block_count, block_rows)

    def one_block(carry_in, inputs):
        return (
            attend_block(
                carry_in,
                inputs[0],
                inputs[1],
                inputs[2],
                query_grid,
                query_pos,
                query_limit,
                score_scale,
            ),
            None,
        )

    carried, unused = lax.scan(one_block, carried, (key_blocks, value_blocks, pos_blocks))
    return carried


def per_device(
    queries, key_rows, value_rows, residual, out_weight, norm_gain, value_head, valid_length
):
    device = lax.axis_index("seq")
    tok_count = queries.shape[0]
    valid_upto = valid_length[0]
    groups = key_rows.shape[1] // HEAD_DIM
    repeats = queries.shape[1] // key_rows.shape[1]
    score_scale = HEAD_DIM ** (-0.5)
    local_rows = jnp.arange(tok_count, dtype=jnp.int32)
    query_pos = row_positions(device * tok_count + local_rows, tok_count)
    query_ok = query_pos < valid_upto
    query_limit = jnp.max(jnp.where(query_ok, query_pos, -1))
    query_grid = queries.reshape(tok_count, groups, repeats, HEAD_DIM)
    start_state = (
        jnp.full((tok_count, groups, repeats), NEG_BIG, jnp.float32),
        jnp.zeros((tok_count, groups, repeats), jnp.float32),
        jnp.zeros((tok_count, groups, repeats, HEAD_DIM), jnp.float32),
    )
    key_piece = lax.all_gather(key_rows, "seq", axis=0, tiled=True)
    key_pos = row_positions(jnp.arange(key_piece.shape[0], dtype=jnp.int32), tok_count)
    carried = attend_piece(
        start_state,
        key_piece,
        lax.all_gather(value_rows, "seq", axis=0, tiled=True),
        key_pos,
        query_grid,
        query_pos,
        query_limit,
        score_scale,
    )
    running_max, running_sum, running_out = carried
    safe_sum = jnp.where(query_ok[:, None, None], running_sum, 1.0)
    attended = jnp.where(query_ok[:, None, None, None], running_out / safe_sum[..., None], 0.0)
    attended = attended.reshape(tok_count, groups * repeats * HEAD_DIM).astype(jnp.bfloat16)
    whole_weight = lax.all_gather(out_weight, "seq", axis=0, tiled=True)
    projected = jnp.dot(attended, whole_weight, preferred_element_type=jnp.float32)
    stream = (residual.astype(jnp.float32) + projected).astype(jnp.bfloat16)
    widened = stream.astype(jnp.float32)
    normed = widened * lax.rsqrt(jnp.mean(widened * widened, axis=-1, keepdims=True) + 1e-06)
    scored = jnp.sum(normed * (norm_gain * value_head)[None, :], axis=-1)
    natural_pos = device * tok_count + local_rows
    scored = jnp.where(natural_pos < valid_upto, scored, 0.0)
    return (stream, scored)


def solution(mesh):
    placed = (
        P(("league", "seq"), None),
        P(("league", "seq"), None),
        P(("league", "seq"), None),
        P(("league", "seq"), None),
        P("seq", None),
        P(),
        P(),
        P("league"),
    )
    return jax.shard_map(
        per_device,
        mesh=mesh,
        in_specs=placed,
        out_specs=(P(("league", "seq"), None), P(("league", "seq"))),
        check_vma=False,
    )
```

profile of v0, /device:TPU:0, one launch (start us, length us, event | category | flops | bytes accessed | tf_op | source)
XLA Modules:
  0.0 211.8 jit_solution(4323758560684722332)
XLA Ops:
  7.2 0.7 all-gather.4.cloned.1.call-update
  8.0 0.7 all-gather.6.cloned.1.call-update
  8.7 0.7 all-gather.8.cloned.1.call-update
  10.1 1.9 reshape.101
  12.9 39.7 %all-gather.4.cloned.1.call-done = bf16[3072,256]{1,0:T(8,128)(2,1)} async-done(((bf16[192,256]{1,0:T(8,128)(2,1)}), bf16[3072,256]{1,0:T(8,128)(2,1)}) %all-gather.4.cloned.1.call-update) | async-done | bytes 1572880 | tf_op jit(solution)/shard_map/all_gather | solution.py:96
  52.6 2.4 %reshape.100 = bf16[6,512,2,128]{3,2,1,0:T(2,128)(2,1)S(1)} reshape(bf16[3072,256]{1,0:T(8,128)(2,1)} %all-gather.4.cloned.1.call-done) | data formatting | bytes 3145728 | tf_op jit(solution)/shard_map/reshape | solution.py:54
  55.0 1.4 copy.10
  56.4 36.8 %all-gather.6.cloned.1.call-done = bf16[3072,256]{1,0:T(8,128)(2,1)} async-done(((bf16[192,256]{1,0:T(8,128)(2,1)}), bf16[3072,256]{1,0:T(8,128)(2,1)}) %all-gather.6.cloned.1.call-update) | async-done | bytes 1572880 | tf_op jit(solution)/shard_map/all_gather | solution.py:101
  93.3 2.4 %reshape.102 = bf16[6,512,2,128]{3,2,1,0:T(2,128)(2,1)S(1)} reshape(bf16[3072,256]{1,0:T(8,128)(2,1)} %all-gather.6.cloned.1.call-done) | data formatting | bytes 3145728 | tf_op jit(solution)/shard_map/reshape | solution.py:55
  95.6 1.4 copy.12
  97.2 19.7 %while.15 = (s32[]{:T(128)}, f32[192,2,7]{0,2,1:T(8,128)S(1)}, f32[192,2,7]{0,2,1:T(8,128)S(1)}, f32[192,2,7,128]{3,0,2,1:T(8,128)S(1)}, s32[6,512]{1,0:T(8,128)...) while((s32[]{:T(128)}, f32[192,2,7]{0,2,1:T(8,128)S(1)}, ...), condition=%wide.region_7.8_spmd.clone, body=%wide.region_1.7_spmd.clone.sunk | while | flops 720577664 | bytes 21064692 | solution.py:73
  97.2 0.7 fusion.52
  99.3 6.9 %conditional.3 = ((f32[192,2,7]{0,2,1:T(8,128)S(1)}, f32[192,2,7]{0,2,1:T(8,128)S(1)}, f32[192,2,7,128]{3,0,2,1:T(8,128)S(1)})) conditional(s32[]{:T(128)} %convert_element_type.48, (f32[192,2,7]{0,2,1:T(8,128)S(1)}, f32[192,2,7]{0,2,1:T(8,128)S(1)}, f32[192,2,7,128]{3,0,2,1:T(8,128)S(1)}) %tuple.53, (s32[1,512]{1,0:T(1,128)S(1)}, ...), branch_computations={%region_3.3_spmd, %region_4.6_spmd.clone} | conditional | flops 720575808 | bytes 21056228 | solution.py:44
  99.5 2.0 fusion.2
  101.5 1.8 fusion.6
  103.3 2.9 %fusion.16 = f32[192,2,7,128]{3,0,2,1:T(8,128)S(1)} fusion(f32[2,512,192,7]{1,2,3,0:T(8,128)S(1)} %get-tuple-element.265, f32[192,2,7]{0,2,1:T(8,128)S(1)} %max.5, pred[192,512]{1,0:T(8,128)(4,1)S(1)} %broadcast_compare_fusion, f32[192,2,7,128]{3,0,2,1:T(8,128)S(1)} %get-tuple-element.208, f32[192,2,7]{0,2,1:T(8,128)S(1)} %get-tuple-element.261, ...), kind=kOutput, calls=%fused_computation.14 | convolution fusion | flops 358514688 | bytes 8640000 | tf_op jit(solution)/shard_map/while/body/eval_jaxpr/cond/branch_1_fun/qgrk,kgd->qgrd/dot_general | solution.py:32
  106.2 0.7 fusion.52
  108.3 0.7 fusion.52
  110.5 0.7 fusion.52
  112.6 0.7 fusion.52
  114.8 0.7 fusion.52
  117.9 0.7 convert_element_type.25
  118.6 77.7 %all-gather.8.cloned.1.call-done = bf16[1792,3584]{1,0:T(8,128)(2,1)} async-done(((bf16[112,3584]{1,0:T(8,128)(2,1)}), bf16[1792,3584]{1,0:T(8,128)(2,1)}) %all-gather.8.cloned.1.call-update) | async-done | bytes 12845072 | tf_op jit(solution)/shard_map/all_gather | solution.py:112
  196.3 7.8 %fusion.35 = (f32[192]{0:T(256)S(1)}, bf16[192,3584]{1,0:T(8,128)(2,1)S(1)}) fusion(bf16[192,1792]{1,0:T(8,128)(2,1)S(1)} %convert_element_type.25, bf16[1792,3584]{1,0:T(8,128)(2,1)} %all-gather.8.cloned.1.call-done, bf16[192,3584]{1,0:T(8,128)(2,1)} %param.15), kind=kOutput, calls=%fused_computation.42 | convolution fusion | flops 2470379264 | bytes 16286464 | tf_op jit(solution)/shard_map/dot_general | solution.py:113
  (63 shorter events, 3.6 us)
Async XLA Ops:
  7.2 5.0 %copy-start.1 = (f32[3584]{0:T(1024)S(1)}, f32[3584]{0:T(1024)}, u32[]{:S(2)}) copy-start(f32[3584]{0:T(1024)} %param.17) | copy-start | bytes 43012
  7.2 5.0 %copy-start.2 = (f32[3584]{0:T(1024)S(1)}, f32[3584]{0:T(1024)}, u32[]{:S(2)}) copy-start(f32[3584]{0:T(1024)} %param.18) | copy-start | bytes 43012
  7.2 45.4 %all-gather.4.cloned.1.call-start = ((), (), s32[]{:S(2)}) async-start(), calls=%async_computation | async-start | bytes 1671168 | tf_op jit(solution)/shard_map/all_gather | solution.py:96
  7.9 85.3 %all-gather.6.cloned.1.call-start = ((), (), s32[]{:S(2)}) async-start(), calls=%async_computation.1 | async-start | bytes 1671168 | tf_op jit(solution)/shard_map/all_gather | solution.py:101
  8.7 187.7 %all-gather.8.cloned.1.call-start = ((), (), s32[]{:S(2)}) async-start(), calls=%async_computation.2 | async-start | bytes 13647872 | tf_op jit(solution)/shard_map/all_gather | solution.py:112
  204.1 1.1 copy-start
Sparse Core Ops, SparseCore 0:
  10.3 42.3 all-gather.3
  54.9 38.2 all-gather.5
  95.5 100.7 all-gather.7
where the time goes:
time: 212 us
  waiting for transfers between devices  156 us (74%)
  between operations  14.6 us (7%)
  matrix products  12.7 us (6%)
  local copies, waits for them, and re-layouts  11 us (5%)
  other arithmetic  8.68 us (4%)
  loops' own time  8.39 us (4%)
    all_gather x1, waiting for transfers between devices, per_device(): whole_weight = lax.all_gather(out_weight, 'seq', axis=0, tiled=True)  77.7 us
    all_gather x1, waiting for transfers between devices, per_device(): key_piece = lax.all_gather(key_rows, 'seq', axis=0, tiled=True)  39.7 us
    all_gather x1, waiting for transfers between devices, per_device(): lax.all_gather(value_rows, 'seq', axis=0, tiled=True)  36.8 us
    another operation x1, loops' own time, attend_piece(): lax.scan(one_block, carried, (key_blocks, value_blocks, pos_blocks))  8.26 us
    dot_general x1, matrix products, per_device(): jnp.dot(attended, whole_weight, preferred_element_type=jnp.float32)  7.8 us
    reduce_min x6, other arithmetic, attend_block(): needed = jnp.min(key_pos) <= query_limit  4.3 us
  transfers between devices with their start and end apart: 3, of which 3 were waited for; matrix products, arithmetic and copies ran while one was open for 11% of the time, Pallas kernels for 0%

commit v1 on v0

--- a/solution.py
+++ b/solution.py
@@ -6,6 +6,16 @@
 
 HEAD_DIM = 128
 NEG_BIG = -1e30
+
+
+def pass_along(x, name, d):
+    n_dev = lax.axis_size(name)
+    moving, blocks = (x, [x])
+    for _ in range(n_dev - 1):
+        moving = lax.ppermute(moving, name, [(i, (i + 1) % n_dev) for i in range(n_dev)])
+        blocks.insert(0, moving)
+    line = jnp.concatenate(blocks, axis=d)
+    return jnp.roll(line, (lax.axis_index(name) + 1) * x.shape[d], axis=d)
 
 
 def row_positions(row_index, tok_count):
@@ -93,7 +103,7 @@
         jnp.zeros((tok_count, groups, repeats), jnp.float32),
         jnp.zeros((tok_count, groups, repeats, HEAD_DIM), jnp.float32),
     )
-    key_piece = lax.all_gather(key_rows, "seq", axis=0, tiled=True)
+    key_piece = pass_along(key_rows, "seq", 0)
     key_pos = row_positions(jnp.arange(key_piece.shape[0], dtype=jnp.int32), tok_count)
     carried = attend_piece(
         start_state,

time: 212 us -> 202 us (0.953)
  the two profiles are of different devices: /device:TPU:0 before, /device:TPU:31 now
where the time goes in v1:
time: 202 us; the launch traced here: 201 us
  starting transfers between devices  72.6 us (36%)
  waiting for transfers between devices  37.7 us (19%)
  matrix products  36.9 us (18%)
  other arithmetic  17.6 us (9%)
  between operations  15.1 us (7%)
  local copies, waits for them, and re-layouts  13 us (6%)
  loops' own time  7.91 us (4%)
    ppermute x15, starting transfers between devices, pass_along(): lax.ppermute(moving, name, [(i, (i + 1) % n_dev) for i in range(n_dev)])  72.5 us
    ppermute x15, waiting for transfers between devices, pass_along(): lax.ppermute(moving, name, [(i, (i + 1) % n_dev) for i in range(n_dev)])  36.3 us
    dot_general x6, matrix products, run_block(): jnp.einsum('qgrk,kgd->qgrd', weights.astype(jnp.bfloat16), value_block, p...  16.9 us
    dot_general x6, matrix products, run_block(): jnp.einsum('qgrd,kgd->qgrk', query_grid, key_block, preferred_element_typ...  12.2 us
    reduce_sum x6, other arithmetic, run_block(): running_sum = running_sum * shrink + jnp.sum(weights, axis=-1)  10.6 us
    dot_general x1, matrix products, per_device(): jnp.dot(attended, whole_weight, preferred_element_type=jnp.float32)  7.8 us
    another operation x1, loops' own time, attend_piece(): lax.scan(one_block, carried, (key_blocks, value_blocks, pos_blocks))  7.54 us
  transfers between devices with their start and end apart: 17, of which 14 were waited for; matrix products, arithmetic and copies ran while one was open for 29% of the time, Pallas kernels for 0%

profile of v1, /device:TPU:31, one launch (start us, length us, event | category | flops | bytes accessed | tf_op | source)
XLA Modules:
  0.0 200.9 jit_solution(17054682914979691447)
XLA Ops:
  11.1 5.0 %collective-permute-start.1 = (bf16[192,256]{1,0:T(8,128)(2,1)S(1)}, bf16[192,256]{1,0:T(8,128)(2,1)S(1)}, u32[]{:S(2)}, u32[]{:S(2)}) collective-permute-start(bf16[192,256]{1,0:T(8,128)(2,1)S(1)} %collective-permute-done), channel_id=1, source_target_pairs={{0,1},{1,2},{2,3},{3,4},{4,5},{5,6},{6,7},{7,8},{8,9},{9,10},{10,1... | collective-permute-start | bytes 294920 | tf_op jit(solution)/shard_map/ppermute | solution.py:15
  17.8 5.1 %collective-permute-start.2 = (bf16[192,256]{1,0:T(8,128)(2,1)S(1)}, bf16[192,256]{1,0:T(8,128)(2,1)S(1)}, u32[]{:S(2)}, u32[]{:S(2)}) collective-permute-start(bf16[192,256]{1,0:T(8,128)(2,1)S(1)} %collective-permute-done.1), channel_id=1, source_target_pairs={{0,1},{1,2},{2,3},{3,4},{4,5},{5,6},{6,7},{7,8},{8,9},{9,10},{10,1... | collective-permute-start | bytes 294920 | tf_op jit(solution)/shard_map/ppermute | solution.py:15
  24.9 5.2 %collective-permute-start.3 = (bf16[192,256]{1,0:T(8,128)(2,1)S(1)}, bf16[192,256]{1,0:T(8,128)(2,1)S(1)}, u32[]{:S(2)}, u32[]{:S(2)}) collective-permute-start(bf16[192,256]{1,0:T(8,128)(2,1)S(1)} %collective-permute-done.2), channel_id=1, source_target_pairs={{0,1},{1,2},{2,3},{3,4},{4,5},{5,6},{6,7},{7,8},{8,9},{9,10},{10,1... | collective-permute-start | bytes 294920 | tf_op jit(solution)/shard_map/ppermute | solution.py:15
  31.7 5.1 %collective-permute-start.4 = (bf16[192,256]{1,0:T(8,128)(2,1)S(1)}, bf16[192,256]{1,0:T(8,128)(2,1)S(1)}, u32[]{:S(2)}, u32[]{:S(2)}) collective-permute-start(bf16[192,256]{1,0:T(8,128)(2,1)S(1)} %collective-permute-done.3), channel_id=1, source_target_pairs={{0,1},{1,2},{2,3},{3,4},{4,5},{5,6},{6,7},{7,8},{8,9},{9,10},{10,1... | collective-permute-start | bytes 294920 | tf_op jit(solution)/shard_map/ppermute | solution.py:15
  40.4 5.2 %collective-permute-start.5 = (bf16[192,256]{1,0:T(8,128)(2,1)S(1)}, bf16[192,256]{1,0:T(8,128)(2,1)S(1)}, u32[]{:S(2)}, u32[]{:S(2)}) collective-permute-start(bf16[192,256]{1,0:T(8,128)(2,1)S(1)} %collective-permute-done.4), channel_id=1, source_target_pairs={{0,1},{1,2},{2,3},{3,4},{4,5},{5,6},{6,7},{7,8},{8,9},{9,10},{10,1... | collective-permute-start | bytes 294920 | tf_op jit(solution)/shard_map/ppermute | solution.py:15
  47.2 5.2 %collective-permute-start.6 = (bf16[192,256]{1,0:T(8,128)(2,1)S(1)}, bf16[192,256]{1,0:T(8,128)(2,1)S(1)}, u32[]{:S(2)}, u32[]{:S(2)}) collective-permute-start(bf16[192,256]{1,0:T(8,128)(2,1)S(1)} %collective-permute-done.5), channel_id=1, source_target_pairs={{0,1},{1,2},{2,3},{3,4},{4,5},{5,6},{6,7},{7,8},{8,9},{9,10},{10,1... | collective-permute-start | bytes 294920 | tf_op jit(solution)/shard_map/ppermute | solution.py:15
  54.1 5.1 %collective-permute-start.7 = (bf16[192,256]{1,0:T(8,128)(2,1)S(1)}, bf16[192,256]{1,0:T(8,128)(2,1)S(1)}, u32[]{:S(2)}, u32[]{:S(2)}) collective-permute-start(bf16[192,256]{1,0:T(8,128)(2,1)S(1)} %collective-permute-done.6), channel_id=1, source_target_pairs={{0,1},{1,2},{2,3},{3,4},{4,5},{5,6},{6,7},{7,8},{8,9},{9,10},{10,1... | collective-permute-start | bytes 294920 | tf_op jit(solution)/shard_map/ppermute | solution.py:15
  60.8 5.2 %collective-permute-start.8 = (bf16[192,256]{1,0:T(8,128)(2,1)S(1)}, bf16[192,256]{1,0:T(8,128)(2,1)S(1)}, u32[]{:S(2)}, u32[]{:S(2)}) collective-permute-start(bf16[192,256]{1,0:T(8,128)(2,1)S(1)} %collective-permute-done.7), channel_id=1, source_target_pairs={{0,1},{1,2},{2,3},{3,4},{4,5},{5,6},{6,7},{7,8},{8,9},{9,10},{10,1... | collective-permute-start | bytes 294920 | tf_op jit(solution)/shard_map/ppermute | solution.py:15
  66.0 3.8 %collective-permute-done.8 = bf16[192,256]{1,0:T(8,128)(2,1)S(1)} collective-permute-done((bf16[192,256]{1,0:T(8,128)(2,1)S(1)}, bf16[192,256]{1,0:T(8,128)(2,1)S(1)}, u32[]{:S(2)}, u32[]{:S(2)}) %collective-permute-start.8) | collective-permute-done | bytes 98336 | tf_op jit(solution)/shard_map/ppermute | solution.py:15
  69.8 5.2 %collective-permute-start.9 = (bf16[192,256]{1,0:T(8,128)(2,1)S(1)}, bf16[192,256]{1,0:T(8,128)(2,1)S(1)}, u32[]{:S(2)}, u32[]{:S(2)}) collective-permute-start(bf16[192,256]{1,0:T(8,128)(2,1)S(1)} %collective-permute-done.8), channel_id=1, source_target_pairs={{0,1},{1,2},{2,3},{3,4},{4,5},{5,6},{6,7},{7,8},{8,9},{9,10},{10,1... | collective-permute-start | bytes 294920 | tf_op jit(solution)/shard_map/ppermute | solution.py:15
  75.0 3.8 %collective-permute-done.9 = bf16[192,256]{1,0:T(8,128)(2,1)S(1)} collective-permute-done((bf16[192,256]{1,0:T(8,128)(2,1)S(1)}, bf16[192,256]{1,0:T(8,128)(2,1)S(1)}, u32[]{:S(2)}, u32[]{:S(2)}) %collective-permute-start.9) | collective-permute-done | bytes 98336 | tf_op jit(solution)/shard_map/ppermute | solution.py:15
  78.8 5.2 %collective-permute-start.10 = (bf16[192,256]{1,0:T(8,128)(2,1)S(1)}, bf16[192,256]{1,0:T(8,128)(2,1)S(1)}, u32[]{:S(2)}, u32[]{:S(2)}) collective-permute-start(bf16[192,256]{1,0:T(8,128)(2,1)S(1)} %collective-permute-done.9), channel_id=1, source_target_pairs={{0,1},{1,2},{2,3},{3,4},{4,5},{5,6},{6,7},{7,8},{8,9},{9,10},{10,1... | collective-permute-start | bytes 294920 | tf_op jit(solution)/shard_map/ppermute | solution.py:15
  87.7 5.2 %collective-permute-start.11 = (bf16[192,256]{1,0:T(8,128)(2,1)S(1)}, bf16[192,256]{1,0:T(8,128)(2,1)S(1)}, u32[]{:S(2)}, u32[]{:S(2)}) collective-permute-start(bf16[192,256]{1,0:T(8,128)(2,1)S(1)} %collective-permute-done.10), channel_id=1, source_target_pairs={{0,1},{1,2},{2,3},{3,4},{4,5},{5,6},{6,7},{7,8},{8,9},{9,10},{10,1... | collective-permute-start | bytes 294920 | tf_op jit(solution)/shard_map/ppermute | solution.py:15
  94.6 5.1 %collective-permute-start.12 = (bf16[192,256]{1,0:T(8,128)(2,1)S(1)}, bf16[192,256]{1,0:T(8,128)(2,1)S(1)}, u32[]{:S(2)}, u32[]{:S(2)}) collective-permute-start(bf16[192,256]{1,0:T(8,128)(2,1)S(1)} %collective-permute-done.11), channel_id=1, source_target_pairs={{0,1},{1,2},{2,3},{3,4},{4,5},{5,6},{6,7},{7,8},{8,9},{9,10},{10,1... | collective-permute-start | bytes 294920 | tf_op jit(solution)/shard_map/ppermute | solution.py:15
  103.3 5.2 %collective-permute-start.13 = (bf16[192,256]{1,0:T(8,128)(2,1)S(1)}, bf16[192,256]{1,0:T(8,128)(2,1)S(1)}, u32[]{:S(2)}, u32[]{:S(2)}) collective-permute-start(bf16[192,256]{1,0:T(8,128)(2,1)S(1)} %collective-permute-done.12), channel_id=1, source_target_pairs={{0,1},{1,2},{2,3},{3,4},{4,5},{5,6},{6,7},{7,8},{8,9},{9,10},{10,1... | collective-permute-start | bytes 294920 | tf_op jit(solution)/shard_map/ppermute | solution.py:15
  112.2 5.2 %collective-permute-start.14 = (bf16[192,256]{1,0:T(8,128)(2,1)S(1)}, bf16[192,256]{1,0:T(8,128)(2,1)S(1)}, u32[]{:S(2)}, u32[]{:S(2)}) collective-permute-start(bf16[192,256]{1,0:T(8,128)(2,1)S(1)} %collective-permute-done.13), channel_id=1, source_target_pairs={{0,1},{1,2},{2,3},{3,4},{4,5},{5,6},{6,7},{7,8},{8,9},{9,10},{10,1... | collective-permute-start | bytes 294920 | tf_op jit(solution)/shard_map/ppermute | solution.py:15
  131.0 52.4 %while.15 = (s32[]{:T(128)}, f32[192,2,7]{0,2,1:T(8,128)S(1)}, f32[192,2,7]{0,2,1:T(8,128)S(1)}, f32[192,2,7,128]{3,0,2,1:T(8,128)S(1)}, s32[6,512]{1,0:T(8,128)...) while((s32[]{:T(128)}, f32[192,2,7]{0,2,1:T(8,128)S(1)}, ...), condition=%wide.region_7.8_spmd.clone, body=%wide.region_1.7_spmd.clone.sunk | while | flops 720577664 | bytes 21064692 | solution.py:83
  132.9 6.8 %conditional.3 = ((f32[192,2,7]{0,2,1:T(8,128)S(1)}, f32[192,2,7]{0,2,1:T(8,128)S(1)}, f32[192,2,7,128]{3,0,2,1:T(8,128)S(1)})) conditional(s32[]{:T(128)} %convert_element_type.48, (f32[192,2,7]{0,2,1:T(8,128)S(1)}, f32[192,2,7]{0,2,1:T(8,128)S(1)}, f32[192,2,7,128]{3,0,2,1:T(8,128)S(1)}) %tuple.53, (s32[1,512]{1,0:T(1,128)S(1)}, ...), branch_computations={%region_3.3_spmd, %region_4.6_spmd.clone} | conditional | flops 720575808 | bytes 21056228 | solution.py:54
  141.6 6.8 %conditional.3 = ((f32[192,2,7]{0,2,1:T(8,128)S(1)}, f32[192,2,7]{0,2,1:T(8,128)S(1)}, f32[192,2,7,128]{3,0,2,1:T(8,128)S(1)})) conditional(s32[]{:T(128)} %convert_element_type.48, (f32[192,2,7]{0,2,1:T(8,128)S(1)}, f32[192,2,7]{0,2,1:T(8,128)S(1)}, f32[192,2,7,128]{3,0,2,1:T(8,128)S(1)}) %tuple.53, (s32[1,512]{1,0:T(1,128)S(1)}, ...), branch_computations={%region_3.3_spmd, %region_4.6_spmd.clone} | conditional | flops 720575808 | bytes 21056228 | solution.py:54
  150.3 6.9 %conditional.3 = ((f32[192,2,7]{0,2,1:T(8,128)S(1)}, f32[192,2,7]{0,2,1:T(8,128)S(1)}, f32[192,2,7,128]{3,0,2,1:T(8,128)S(1)})) conditional(s32[]{:T(128)} %convert_element_type.48, (f32[192,2,7]{0,2,1:T(8,128)S(1)}, f32[192,2,7]{0,2,1:T(8,128)S(1)}, f32[192,2,7,128]{3,0,2,1:T(8,128)S(1)}) %tuple.53, (s32[1,512]{1,0:T(1,128)S(1)}, ...), branch_computations={%region_3.3_spmd, %region_4.6_spmd.clone} | conditional | flops 720575808 | bytes 21056228 | solution.py:54
  159.2 6.8 %conditional.3 = ((f32[192,2,7]{0,2,1:T(8,128)S(1)}, f32[192,2,7]{0,2,1:T(8,128)S(1)}, f32[192,2,7,128]{3,0,2,1:T(8,128)S(1)})) conditional(s32[]{:T(128)} %convert_element_type.48, (f32[192,2,7]{0,2,1:T(8,128)S(1)}, f32[192,2,7]{0,2,1:T(8,128)S(1)}, f32[192,2,7,128]{3,0,2,1:T(8,128)S(1)}) %tuple.53, (s32[1,512]{1,0:T(1,128)S(1)}, ...), branch_computations={%region_3.3_spmd, %region_4.6_spmd.clone} | conditional | flops 720575808 | bytes 21056228 | solution.py:54
  167.9 6.8 %conditional.3 = ((f32[192,2,7]{0,2,1:T(8,128)S(1)}, f32[192,2,7]{0,2,1:T(8,128)S(1)}, f32[192,2,7,128]{3,0,2,1:T(8,128)S(1)})) conditional(s32[]{:T(128)} %convert_element_type.48, (f32[192,2,7]{0,2,1:T(8,128)S(1)}, f32[192,2,7]{0,2,1:T(8,128)S(1)}, f32[192,2,7,128]{3,0,2,1:T(8,128)S(1)}) %tuple.53, (s32[1,512]{1,0:T(1,128)S(1)}, ...), branch_computations={%region_3.3_spmd, %region_4.6_spmd.clone} | conditional | flops 720575808 | bytes 21056228 | solution.py:54
  176.6 6.8 %conditional.3 = ((f32[192,2,7]{0,2,1:T(8,128)S(1)}, f32[192,2,7]{0,2,1:T(8,128)S(1)}, f32[192,2,7,128]{3,0,2,1:T(8,128)S(1)})) conditional(s32[]{:T(128)} %convert_element_type.48, (f32[192,2,7]{0,2,1:T(8,128)S(1)}, f32[192,2,7]{0,2,1:T(8,128)S(1)}, f32[192,2,7,128]{3,0,2,1:T(8,128)S(1)}) %tuple.53, (s32[1,512]{1,0:T(1,128)S(1)}, ...), branch_computations={%region_3.3_spmd, %region_4.6_spmd.clone} | conditional | flops 720575808 | bytes 21056228 | solution.py:54
  185.2 7.8 %fusion.35 = (f32[192]{0:T(256)S(1)}, bf16[192,3584]{1,0:T(8,128)(2,1)S(1)}) fusion(bf16[192,1792]{1,0:T(8,128)(2,1)S(1)} %convert_element_type.25, bf16[1792,3584]{1,0:T(8,128)(2,1)} %all-gather.5.cloned.1.call-done, bf16[192,3584]{1,0:T(8,128)(2,1)} %param.15), kind=kOutput, calls=%fused_computation.42 | convolution fusion | flops 2470379264 | bytes 16286464 | tf_op jit(solution)/shard_map/dot_general | solution.py:123
  (165 shorter events, 90.4 us)
Async XLA Ops:
  7.2 95.4 %copy-start.2 = (f32[3584]{0:T(1024)S(1)}, f32[3584]{0:T(1024)}, u32[]{:S(2)}) copy-start(f32[3584]{0:T(1024)} %param.17) | copy-start | bytes 43012
  7.2 95.4 %copy-start.3 = (f32[3584]{0:T(1024)S(1)}, f32[3584]{0:T(1024)}, u32[]{:S(2)}) copy-start(f32[3584]{0:T(1024)} %param.18) | copy-start | bytes 43012
  7.2 119.9 %all-gather.3.cloned.1.call-start = ((), (), s32[]{:S(2)}) async-start(), calls=%async_computation | async-start | bytes 1671168 | tf_op jit(solution)/shard_map/all_gather | solution.py:111
  7.9 177.2 %all-gather.5.cloned.1.call-start = ((), (), s32[]{:S(2)}) async-start(), calls=%async_computation.1 | async-start | bytes 13647872 | tf_op jit(solution)/shard_map/all_gather | solution.py:122
  8.7 112.8 %copy-start.1 = (bf16[192,256]{1,0:T(8,128)(2,1)S(1)}, bf16[192,256]{1,0:T(8,128)(2,1)}, u32[]{:S(2)}) copy-start(bf16[192,256]{1,0:T(8,128)(2,1)} %param.13) | copy-start | bytes 294916
  8.7 2.5 %collective-permute-start = (bf16[192,256]{1,0:T(8,128)(2,1)}, bf16[192,256]{1,0:T(8,128)(2,1)S(1)}, u32[]{:S(2)}, u32[]{:S(2)}) collective-permute-start(bf16[192,256]{1,0:T(8,128)(2,1)} %param.13), channel_id=1, source_target_pairs={{0,1},{1,2},{2,3},{3,4},{4,5},{5,6},{6,7},{7,8},{8,9},{9,10},{10,1... | collective-permute-start | bytes 294920 | tf_op jit(solution)/shard_map/ppermute | solution.py:15
  11.1 6.6 %collective-permute-start.1 = (bf16[192,256]{1,0:T(8,128)(2,1)S(1)}, bf16[192,256]{1,0:T(8,128)(2,1)S(1)}, u32[]{:S(2)}, u32[]{:S(2)}) collective-permute-start(bf16[192,256]{1,0:T(8,128)(2,1)S(1)} %collective-permute-done), channel_id=1, source_target_pairs={{0,1},{1,2},{2,3},{3,4},{4,5},{5,6},{6,7},{7,8},{8,9},{9,10},{10,1... | collective-permute-start | bytes 294920 | tf_op jit(solution)/shard_map/ppermute | solution.py:15
  17.8 7.1 %collective-permute-start.2 = (bf16[192,256]{1,0:T(8,128)(2,1)S(1)}, bf16[192,256]{1,0:T(8,128)(2,1)S(1)}, u32[]{:S(2)}, u32[]{:S(2)}) collective-permute-start(bf16[192,256]{1,0:T(8,128)(2,1)S(1)} %collective-permute-done.1), channel_id=1, source_target_pairs={{0,1},{1,2},{2,3},{3,4},{4,5},{5,6},{6,7},{7,8},{8,9},{9,10},{10,1... | collective-permute-start | bytes 294920 | tf_op jit(solution)/shard_map/ppermute | solution.py:15
  24.9 6.8 %collective-permute-start.3 = (bf16[192,256]{1,0:T(8,128)(2,1)S(1)}, bf16[192,256]{1,0:T(8,128)(2,1)S(1)}, u32[]{:S(2)}, u32[]{:S(2)}) collective-permute-start(bf16[192,256]{1,0:T(8,128)(2,1)S(1)} %collective-permute-done.2), channel_id=1, source_target_pairs={{0,1},{1,2},{2,3},{3,4},{4,5},{5,6},{6,7},{7,8},{8,9},{9,10},{10,1... | collective-permute-start | bytes 294920 | tf_op jit(solution)/shard_map/ppermute | solution.py:15
  31.7 8.6 %collective-permute-start.4 = (bf16[192,256]{1,0:T(8,128)(2,1)S(1)}, bf16[192,256]{1,0:T(8,128)(2,1)S(1)}, u32[]{:S(2)}, u32[]{:S(2)}) collective-permute-start(bf16[192,256]{1,0:T(8,128)(2,1)S(1)} %collective-permute-done.3), channel_id=1, source_target_pairs={{0,1},{1,2},{2,3},{3,4},{4,5},{5,6},{6,7},{7,8},{8,9},{9,10},{10,1... | collective-permute-start | bytes 294920 | tf_op jit(solution)/shard_map/ppermute | solution.py:15
  40.4 6.9 %collective-permute-start.5 = (bf16[192,256]{1,0:T(8,128)(2,1)S(1)}, bf16[192,256]{1,0:T(8,128)(2,1)S(1)}, u32[]{:S(2)}, u32[]{:S(2)}) collective-permute-start(bf16[192,256]{1,0:T(8,128)(2,1)S(1)} %collective-permute-done.4), channel_id=1, source_target_pairs={{0,1},{1,2},{2,3},{3,4},{4,5},{5,6},{6,7},{7,8},{8,9},{9,10},{10,1... | collective-permute-start | bytes 294920 | tf_op jit(solution)/shard_map/ppermute | solution.py:15
  47.2 6.8 %collective-permute-start.6 = (bf16[192,256]{1,0:T(8,128)(2,1)S(1)}, bf16[192,256]{1,0:T(8,128)(2,1)S(1)}, u32[]{:S(2)}, u32[]{:S(2)}) collective-permute-start(bf16[192,256]{1,0:T(8,128)(2,1)S(1)} %collective-permute-done.5), channel_id=1, source_target_pairs={{0,1},{1,2},{2,3},{3,4},{4,5},{5,6},{6,7},{7,8},{8,9},{9,10},{10,1... | collective-permute-start | bytes 294920 | tf_op jit(solution)/shard_map/ppermute | solution.py:15
  54.1 6.7 %collective-permute-start.7 = (bf16[192,256]{1,0:T(8,128)(2,1)S(1)}, bf16[192,256]{1,0:T(8,128)(2,1)S(1)}, u32[]{:S(2)}, u32[]{:S(2)}) collective-permute-start(bf16[192,256]{1,0:T(8,128)(2,1)S(1)} %collective-permute-done.6), channel_id=1, source_target_pairs={{0,1},{1,2},{2,3},{3,4},{4,5},{5,6},{6,7},{7,8},{8,9},{9,10},{10,1... | collective-permute-start | bytes 294920 | tf_op jit(solution)/shard_map/ppermute | solution.py:15
  60.8 9.0 %collective-permute-start.8 = (bf16[192,256]{1,0:T(8,128)(2,1)S(1)}, bf16[192,256]{1,0:T(8,128)(2,1)S(1)}, u32[]{:S(2)}, u32[]{:S(2)}) collective-permute-start(bf16[192,256]{1,0:T(8,128)(2,1)S(1)} %collective-permute-done.7), channel_id=1, source_target_pairs={{0,1},{1,2},{2,3},{3,4},{4,5},{5,6},{6,7},{7,8},{8,9},{9,10},{10,1... | collective-permute-start | bytes 294920 | tf_op jit(solution)/shard_map/ppermute | solution.py:15
  69.8 9.0 %collective-permute-start.9 = (bf16[192,256]{1,0:T(8,128)(2,1)S(1)}, bf16[192,256]{1,0:T(8,128)(2,1)S(1)}, u32[]{:S(2)}, u32[]{:S(2)}) collective-permute-start(bf16[192,256]{1,0:T(8,128)(2,1)S(1)} %collective-permute-done.8), channel_id=1, source_target_pairs={{0,1},{1,2},{2,3},{3,4},{4,5},{5,6},{6,7},{7,8},{8,9},{9,10},{10,1... | collective-permute-start | bytes 294920 | tf_op jit(solution)/shard_map/ppermute | solution.py:15
  78.8 9.0 %collective-permute-start.10 = (bf16[192,256]{1,0:T(8,128)(2,1)S(1)}, bf16[192,256]{1,0:T(8,128)(2,1)S(1)}, u32[]{:S(2)}, u32[]{:S(2)}) collective-permute-start(bf16[192,256]{1,0:T(8,128)(2,1)S(1)} %collective-permute-done.9), channel_id=1, source_target_pairs={{0,1},{1,2},{2,3},{3,4},{4,5},{5,6},{6,7},{7,8},{8,9},{9,10},{10,1... | collective-permute-start | bytes 294920 | tf_op jit(solution)/shard_map/ppermute | solution.py:15
  87.7 6.8 %collective-permute-start.11 = (bf16[192,256]{1,0:T(8,128)(2,1)S(1)}, bf16[192,256]{1,0:T(8,128)(2,1)S(1)}, u32[]{:S(2)}, u32[]{:S(2)}) collective-permute-start(bf16[192,256]{1,0:T(8,128)(2,1)S(1)} %collective-permute-done.10), channel_id=1, source_target_pairs={{0,1},{1,2},{2,3},{3,4},{4,5},{5,6},{6,7},{7,8},{8,9},{9,10},{10,1... | collective-permute-start | bytes 294920 | tf_op jit(solution)/shard_map/ppermute | solution.py:15
  94.6 8.7 %collective-permute-start.12 = (bf16[192,256]{1,0:T(8,128)(2,1)S(1)}, bf16[192,256]{1,0:T(8,128)(2,1)S(1)}, u32[]{:S(2)}, u32[]{:S(2)}) collective-permute-start(bf16[192,256]{1,0:T(8,128)(2,1)S(1)} %collective-permute-done.11), channel_id=1, source_target_pairs={{0,1},{1,2},{2,3},{3,4},{4,5},{5,6},{6,7},{7,8},{8,9},{9,10},{10,1... | collective-permute-start | bytes 294920 | tf_op jit(solution)/shard_map/ppermute | solution.py:15
  103.3 9.0 %collective-permute-start.13 = (bf16[192,256]{1,0:T(8,128)(2,1)S(1)}, bf16[192,256]{1,0:T(8,128)(2,1)S(1)}, u32[]{:S(2)}, u32[]{:S(2)}) collective-permute-start(bf16[192,256]{1,0:T(8,128)(2,1)S(1)} %collective-permute-done.12), channel_id=1, source_target_pairs={{0,1},{1,2},{2,3},{3,4},{4,5},{5,6},{6,7},{7,8},{8,9},{9,10},{10,1... | collective-permute-start | bytes 294920 | tf_op jit(solution)/shard_map/ppermute | solution.py:15
  112.2 9.0 %collective-permute-start.14 = (bf16[192,256]{1,0:T(8,128)(2,1)S(1)}, bf16[192,256]{1,0:T(8,128)(2,1)S(1)}, u32[]{:S(2)}, u32[]{:S(2)}) collective-permute-start(bf16[192,256]{1,0:T(8,128)(2,1)S(1)} %collective-permute-done.13), channel_id=1, source_target_pairs={{0,1},{1,2},{2,3},{3,4},{4,5},{5,6},{6,7},{7,8},{8,9},{9,10},{10,1... | collective-permute-start | bytes 294920 | tf_op jit(solution)/shard_map/ppermute | solution.py:15
  193.0 1.1 copy-start
Sparse Core Ops, SparseCore 0:
  10.3 39.1 all-gather.2
  51.7 104.6 all-gather.4
